TPU v7x, 128 devices: a whole 4x4x4 slice. The times are simulated.
128 devices in a mesh: walk: 8 (over y, z_hi), chol: 16 (over z_lo, x, core).
Axes of the slice: x: 4, y: 4, z: 4 (z_hi: 2, z_lo: 2; z = z_hi * 2 + z_lo), core: 2. Of those that a mesh axis runs over, the one named last changes fastest.
Arguments:
- orbitals: bfloat16 [1024, 64, 1024], P(('walk', 'chol')), may hold values from -6 to 6
- cholesky: bfloat16 [192, 64, 1024], P('chol'), may hold values from -0.1875 to 0.1875
- parents: int32 [1024], P(('walk', 'chol')), may hold values from 0 to 1023, as said below
- counts: int32 [8, 16], P('walk', 'chol'), may hold values from 1 to 8, as said below
- steps: bfloat16 [1024, 64, 1024], P(('walk', 'chol')), may hold values from -6 to 6
Outputs:
- energy: float32 [1024], P(('walk', 'chol'))
- parent_grad: float32 [1024, 64, 1024], P(('walk', 'chol'))
Inputs may be any that keep to these rules, and one draw needn't show every extreme that they name: The parent of a new walker lies on the same index of chol as the walker. Of one device's new walkers at most 2 have parents on any one index of walk, and on some index exactly 2. The first counts entries of a device's 8 new walkers are live; in every draw some device is full.
All inputs are finite; a program needn't handle non-finite values.
Results may differ from a plain program's by a relative error of at most 0.0044.
Values may be sent and summed in bfloat16 or wider, within the bound.
A program may use at most 128 MiB of HBM per device.

v0:
```python
import jax
import jax.numpy as jnp
from jax import lax
from jax.sharding import Mesh
from jax.sharding import PartitionSpec as P

CAP = 2
WALK = ("walk_0", "walk_1")
WALK_CHOL = ("walk_0", "walk_1", "chol")


def cut_along(shard, dim, devices):
    before, after = (shard.shape[:dim], shard.shape[dim + 1 :])
    return jnp.moveaxis(shard.reshape(*before, devices, -1, *after), dim, 0)


def in_order(parts, dim):
    shape = list(parts.shape[1:])
    shape[dim] *= parts.shape[0]
    return jnp.moveaxis(parts, 0, dim).reshape(shape)


def turned_blocks(parts, axes, sequence):
    shape = [lax.axis_size(a) for a in axes]
    parts = parts.reshape(*shape, *parts.shape[1:])
    for k in sequence:
        parts = lax.all_to_all(parts, axes[k], split_axis=k, concat_axis=k, tiled=True)
    return parts.reshape(-1, *parts.shape[len(axes) :])


def one_axis_at_a_time(shard, axes, sequence, split_dim, concat_dim):
    parts = cut_along(shard, split_dim, lax.axis_size(axes))
    return in_order(turned_blocks(parts, axes, sequence), concat_dim)


def body(orbitals, cholesky, parents, counts, steps):
    walk_size = lax.axis_size(WALK)
    chol_size = lax.axis_size("chol")
    per_device = orbitals.shape[0]
    electrons = orbitals.shape[1]
    basis_len = orbitals.shape[2]
    vectors_dev = cholesky.shape[0]
    source_walk = parents // (chol_size * per_device)
    source_slot = parents % per_device
    position = jnp.arange(per_device, dtype=jnp.int32)
    earlier_same = (source_walk[:, None] == source_walk[None, :]) & (
        position[None, :] < position[:, None]
    )
    rank_within = jnp.sum(earlier_same.astype(jnp.int32), axis=1)
    slot_ids = source_walk * CAP + rank_within
    flat_slots = jnp.arange(walk_size * CAP, dtype=jnp.int32)
    matching = slot_ids[:, None] == flat_slots[None, :]
    wanted = jnp.sum(matching.astype(jnp.int32) * (source_slot[:, None] + 1), axis=0) - 1
    asked = one_axis_at_a_time(wanted.reshape(walk_size, CAP), WALK, (0, 1), 0, 0).reshape(-1)
    picker = (asked[:, None] == position[None, :]).astype(jnp.bfloat16)
    outgoing = jnp.dot(picker, orbitals.reshape(per_device, -1), preferred_element_type=jnp.float32)
    outgoing = outgoing.astype(jnp.bfloat16).reshape(walk_size, CAP, electrons, basis_len)
    incoming = lax.all_to_all(outgoing, WALK, split_axis=0, concat_axis=0, tiled=True)
    gathered = jnp.dot(
        matching.astype(jnp.bfloat16),
        incoming.reshape(walk_size * CAP, -1),
        preferred_element_type=jnp.float32,
    )
    clones = gathered + steps.reshape(per_device, -1).astype(jnp.float32)
    clones = clones.astype(jnp.bfloat16).reshape(per_device, electrons, basis_len)
    piece = lax.all_gather(cholesky, "chol", axis=0, tiled=True)
    shards = piece.shape[0] // vectors_dev
    blocks = piece.reshape(shards, vectors_dev, electrons, basis_len)
    intersection = jnp.einsum(
        "sgip,wjp->swgij", blocks, clones, preferred_element_type=jnp.float32
    ).astype(jnp.bfloat16)
    part = -jnp.einsum("swgji,sgip->swjp", intersection, blocks, preferred_element_type=jnp.float32)
    part = lax.optimization_barrier(part.astype(jnp.bfloat16))
    gradient = jnp.sum(part.astype(jnp.float32), axis=0)
    alive = (position < counts.reshape(-1)[0]).astype(jnp.float32)
    gradient = gradient * alive[:, None, None]
    energy = 0.5 * jnp.sum(clones.astype(jnp.float32) * gradient, axis=(1, 2))
    backward = jnp.dot(
        matching.T.astype(jnp.float32),
        gradient.reshape(per_device, -1),
        precision=lax.Precision.HIGHEST,
    )
    backward = backward.reshape(walk_size, CAP, electrons, basis_len)
    returned = lax.all_to_all(backward, WALK, split_axis=0, concat_axis=0, tiled=True)
    owner = (asked[None, :] == position[:, None]).astype(jnp.float32)
    parent_grad = jnp.dot(
        owner, returned.reshape(walk_size * CAP, -1), precision=lax.Precision.HIGHEST
    )
    return (energy, parent_grad.reshape(per_device, electrons, basis_len))


def solution(mesh):
    torus = Mesh(mesh.devices.reshape(4, 2, mesh.shape["chol"]), ("walk_0", "walk_1", "chol"))
    return jax.shard_map(
        body,
        mesh=torus,
        in_specs=(
            P(WALK_CHOL, None, None),
            P("chol", None, None),
            P(WALK_CHOL),
            P(WALK, "chol"),
            P(WALK_CHOL, None, None),
        ),
        out_specs=(P(WALK_CHOL), P(WALK_CHOL, None, None)),
        check_vma=False,
    )
```

profile of v0, /device:TPU:0, one launch (start us, length us, event | category | flops | bytes accessed | tf_op | source)
XLA Modules:
  0.0 311.1 jit_solution(2648531284516923733)
XLA Ops:
  7.2 0.7 all-gather.2.cloned.1.call-update
  7.9 0.7 and_select_fusion.1
  8.6 0.2 convert_reduce_fusion.1
  8.8 0.1 select_reduce_fusion
  8.9 0.7 sub.11
  9.5 4.6 %all-to-all-start = ((s32[4,2,1,2]{3,1,2,0:T(2,128)}), s32[4,2,1,2]{3,1,2,0:T(2,128)S(1)}, u32[]{:S(2)}, u32[]{:S(2)}) async-start(s32[4,2,1,2]{3,1,2,0:T(2,128)} %bitcast), calls=%async_computation | async-start | bytes 8192 | tf_op jit(solution)/shard_map/all_to_all | solution.py:27
  14.1 0.6 copy.35
  14.7 4.7 %all-to-all-done = s32[4,2,1,2]{3,1,2,0:T(2,128)S(1)} async-done(((s32[4,2,1,2]{3,1,2,0:T(2,128)}), s32[4,2,1,2]{3,1,2,0:T(2,128)S(1)}, u32[]{:S(2)}, u32[]{:S(2)}) %all-to-all-start) | async-done | bytes 96 | tf_op jit(solution)/shard_map/all_to_all | solution.py:27
  19.4 0.1 copy.20
  19.5 10.4 %all_to_all.20 = s32[4,2,1,2]{0,3,2,1:T(2,128)S(1)} all-to-all(s32[4,2,1,2]{0,3,2,1:T(2,128)S(1)} %copy.20), channel_id=1, replica_groups=mesh['walk_0'=4,'walk_1'=2,'chol'=16] {'walk_1'}, dimensions={1} | all-to-all | bytes 128 | tf_op jit(solution)/shard_map/all_to_all | solution.py:27
  29.9 0.1 copy.21
  30.1 0.8 convolution_convert_fusion
  30.8 2.5 copy.36
  33.4 3.7 %all-to-all-start.2 = ((bf16[8,2,64,1024]{3,2,1,0:T(8,128)(2,1)}), bf16[8,2,64,1024]{3,2,1,0:T(8,128)(2,1)S(1)}, u32[]{:S(2)}, u32[]{:S(2)}) async-start(bf16[8,2,64,1024]{3,2,1,0:T(8,128)(2,1)} %bitcast.74), calls=%async_computation.2 | async-start | bytes 4194304 | tf_op jit(solution)/shard_map/all_to_all | solution.py:58
  37.1 0.2 convert_bitcast_fusion
  37.4 2.5 copy.38
  40.6 27.5 %all-to-all-done.2 = bf16[8,2,64,1024]{3,2,1,0:T(8,128)(2,1)S(1)} async-done(((bf16[8,2,64,1024]{3,2,1,0:T(8,128)(2,1)}), bf16[8,2,64,1024]{3,2,1,0:T(8,128)(2,1)S(1)}, u32[]{:S(2)}, u32[]{:S(2)}) %all-to-all-start.2) | async-done | bytes 2097184 | tf_op jit(solution)/shard_map/all_to_all | solution.py:58
  68.1 1.2 copy.37
  69.2 0.5 copy-done
  69.7 0.5 fusion
  70.2 95.6 %all-gather.2.cloned.1.call-done = bf16[192,64,1024]{2,1,0:T(8,128)(2,1)} async-done(((bf16[12,64,1024]{2,1,0:T(8,128)(2,1)}), bf16[192,64,1024]{2,1,0:T(8,128)(2,1)}) %all-gather.2.cloned.1.call-update) | async-done | bytes 25165840 | tf_op jit(solution)/shard_map/all_gather | solution.py:66
  165.8 47.6 %fusion.1 = bf16[16,8,64,1024]{3,2,1,0:T(8,128)(2,1)} fusion(bf16[16,12,64,1024,1]{3,2,1,4,0:T(8,128)(2,1)} %bitcast.83, bf16[8,64,1024,1,1]{2,0,1,4,3:T(8,128)(2,1)S(1)} %bitcast.81), kind=kOutput, calls=%fused_computation.4 | convolution fusion | flops 25792872448 | bytes 42991616 | tf_op jit(solution)/shard_map/swgji,sgip->swjp/dot_general | solution.py:72
  213.4 7.3 %convert_reduce_fusion = f32[8,64,1024]{2,1,0:T(8,128)S(1)} fusion(bf16[16,8,64,1024]{3,2,1,0:T(8,128)(2,1)} %fusion.1), kind=kLoop, calls=%fused_computation.5 | loop fusion | flops 16252928 | bytes 18874368 | tf_op jit(solution)/shard_map/reduce_sum | solution.py:74
  220.8 1.2 copy.39
  222.0 0.9 multiply_reduce_fusion
  222.9 1.8 fusion.14
  224.8 4.4 %copy.24 = f32[8,2,64,1024]{3,2,1,0:T(8,128)} copy(f32[8,2,64,1024]{3,0,2,1:T(8,128)S(1)} %fusion.14) | data formatting | bytes 8388608 | tf_op jit(solution)/shard_map/dot_general | solution.py:78
  229.2 6.6 %all-to-all-start.3 = ((f32[8,2,64,1024]{3,2,1,0:T(8,128)}), f32[8,2,64,1024]{3,2,1,0:T(8,128)}, u32[]{:S(2)}, u32[]{:S(2)}) async-start(f32[8,2,64,1024]{3,2,1,0:T(8,128)} %copy.24), calls=%async_computation.3 | async-start | bytes 8388608 | tf_op jit(solution)/shard_map/all_to_all | solution.py:84
  235.8 0.5 broadcast_multiply_fusion.1
  236.3 59.5 %all-to-all-done.3 = f32[8,2,64,1024]{3,2,1,0:T(8,128)} async-done(((f32[8,2,64,1024]{3,2,1,0:T(8,128)}), f32[8,2,64,1024]{3,2,1,0:T(8,128)}, u32[]{:S(2)}, u32[]{:S(2)}) %all-to-all-start.3) | async-done | bytes 4194336 | tf_op jit(solution)/shard_map/all_to_all | solution.py:84
  295.8 5.9 %fusion.9 = f32[8,64,1024]{2,0,1:T(8,128)S(1)} fusion(s32[16]{0:T(128)S(1)} %eq.84, f32[2,8,64,1024]{3,2,1,0:T(8,128)} %bitcast.39), kind=kOutput, calls=%fused_computation.10 | convolution fusion | flops 100663424 | bytes 6291520 | tf_op jit(solution)/shard_map/dot_general | solution.py:86
  301.7 2.5 copy.26
  (11 shorter events, 0.2 us)
Async XLA Ops:
  7.2 7.0 %copy-start.2 = (bf16[8,64,1024]{2,1,0:T(8,128)(2,1)S(1)}, bf16[8,64,1024]{2,1,0:T(8,128)(2,1)}, u32[]{:S(2)}) copy-start(bf16[8,64,1024]{2,1,0:T(8,128)(2,1)} %param.5) | copy-start | bytes 3145732
  7.2 158.6 %all-gather.2.cloned.1.call-start = ((), (), s32[]{:S(2)}) async-start(), calls=%async_computation.4 | async-start | bytes 26738688 | tf_op jit(solution)/shard_map/all_gather | solution.py:66
  9.5 9.9 %all-to-all-start = ((s32[4,2,1,2]{3,1,2,0:T(2,128)}), s32[4,2,1,2]{3,1,2,0:T(2,128)S(1)}, u32[]{:S(2)}, u32[]{:S(2)}) async-start(s32[4,2,1,2]{3,1,2,0:T(2,128)} %bitcast), calls=%async_computation | async-start | bytes 8192 | tf_op jit(solution)/shard_map/all_to_all | solution.py:27
  33.4 3.7 %copy-start.1 = (bf16[8,64,1024]{2,1,0:T(8,128)(2,1)S(1)}, bf16[8,64,1024]{2,1,0:T(8,128)(2,1)}, u32[]{:S(2)}) copy-start(bf16[8,64,1024]{2,1,0:T(8,128)(2,1)} %param.9) | copy-start | bytes 3145732
  33.4 34.7 %all-to-all-start.2 = ((bf16[8,2,64,1024]{3,2,1,0:T(8,128)(2,1)}), bf16[8,2,64,1024]{3,2,1,0:T(8,128)(2,1)S(1)}, u32[]{:S(2)}, u32[]{:S(2)}) async-start(bf16[8,2,64,1024]{3,2,1,0:T(8,128)(2,1)} %bitcast.74), calls=%async_computation.2 | async-start | bytes 4194304 | tf_op jit(solution)/shard_map/all_to_all | solution.py:58
  68.1 1.6 copy-start
  229.2 66.6 %all-to-all-start.3 = ((f32[8,2,64,1024]{3,2,1,0:T(8,128)}), f32[8,2,64,1024]{3,2,1,0:T(8,128)}, u32[]{:S(2)}, u32[]{:S(2)}) async-start(f32[8,2,64,1024]{3,2,1,0:T(8,128)} %copy.24), calls=%async_computation.3 | async-start | bytes 8388608 | tf_op jit(solution)/shard_map/all_to_all | solution.py:84
Sparse Core Ops, SparseCore 0:
  9.7 156.0 all-gather.1
where the time goes:
time: 312 us; the launch traced here: 311 us
  waiting for transfers between devices  188 us (60%)
  matrix products  56.6 us (18%)
  local copies, waits for them, and re-layouts  16.4 us (5%)
  starting transfers between devices  14.9 us (5%)
  between operations  14.8 us (5%)
  blocking collectives  10.4 us (3%)
  other arithmetic  9.99 us (3%)
    all_gather x1, waiting for transfers between devices, body(): piece = lax.all_gather(cholesky, 'chol', axis=0, tiled=True)  95.6 us
    all_to_all x1, waiting for transfers between devices, body(): lax.all_to_all(backward, WALK, split_axis=0, concat_axis=0, tiled=True)  59.5 us
    dot_general x1, matrix products, body(): jnp.einsum('swgji,sgip->swjp', intersection, blocks, preferred_element_ty...  47.6 us
    all_to_all x1, waiting for transfers between devices, body(): lax.all_to_all(outgoing, WALK, split_axis=0, concat_axis=0, tiled=True)  27.5 us
    unnamed x12, local copies, waits for them, and re-layouts  11 us
    all_to_all x1, blocking collectives, turned_blocks(): lax.all_to_all(parts, axes[k], split_axis=k, concat_axis=k, tiled=True)  10.4 us
    reduce_sum x1, other arithmetic, body(): gradient = jnp.sum(part.astype(jnp.float32), axis=0)  7.34 us
    all_to_all x1, starting transfers between devices, body(): lax.all_to_all(backward, WALK, split_axis=0, concat_axis=0, tiled=True)  6.59 us
  transfers between devices with their start and end apart: 4, of which 4 were waited for; matrix products, arithmetic and copies ran while one was open for 3% of the time, Pallas kernels for 0%

commit v1 on v0

--- a/solution.py
+++ b/solution.py
@@ -63,7 +63,9 @@
     )
     clones = gathered + steps.reshape(per_device, -1).astype(jnp.float32)
     clones = clones.astype(jnp.bfloat16).reshape(per_device, electrons, basis_len)
-    piece = lax.all_gather(cholesky, "chol", axis=0, tiled=True)
+    piece = jnp.concatenate(
+        lax.all_to_all(jnp.stack([cholesky] * lax.axis_size("chol")), "chol", 0, 0), axis=0
+    )
     shards = piece.shape[0] // vectors_dev
     blocks = piece.reshape(shards, vectors_dev, electrons, basis_len)
     intersection = jnp.einsum(

time: 312 us -> 541 us (1.73)
  waiting for transfers between devices: 188 us -> 395 us
  blocking collectives: 10.4 us -> 38.3 us
  between operations: 14.8 us -> 1.4 us
  local copies, waits for them, and re-layouts: 16.4 us -> 23 us
    all_to_all x1, waiting for transfers between devices: 27.5 us -> 333 us  [body(): lax.all_to_all(jnp.stack([cholesky] * lax.axis_size('chol')), 'chol', 0, 0)]
    all_gather x1 -> x0, waiting for transfers between devices: 95.6 us -> none  [body(): piece = lax.all_gather(cholesky, 'chol', axis=0, tiled=True)]
    all_to_all x0 -> x1, blocking collectives: none -> 28.1 us  [body(): lax.all_to_all(outgoing, WALK, split_axis=0, concat_axis=0, tiled=True)]
    another operation x0 -> x1, local copies, waits for them, and re-layouts: none -> 8.55 us  [body(): jnp.stack([cholesky] * lax.axis_size('chol'))]
    unnamed x12 -> x10, local copies, waits for them, and re-layouts: 11 us -> 9.09 us
  transfers between devices with their start and end apart: 4 -> 3, of which waited for: 4 -> 3; matrix products, arithmetic and copies ran while one was open for 3% -> 1% of each run, Pallas kernels for 0% -> 0%
where the time goes in v1:
time: 541 us; the launch traced here: 540 us
  waiting for transfers between devices  395 us (73%)
  matrix products  56.7 us (10%)
  blocking collectives  38.3 us (7%)
  local copies, waits for them, and re-layouts  23 us (4%)
  starting transfers between devices  14.8 us (3%)
  other arithmetic  9.99 us (2%)
    all_to_all x1, waiting for transfers between devices, body(): lax.all_to_all(jnp.stack([cholesky] * lax.axis_size('chol')), 'chol', 0, 0)  333 us
    all_to_all x1, waiting for transfers between devices, body(): lax.all_to_all(backward, WALK, split_axis=0, concat_axis=0, tiled=True)  59.3 us
    dot_general x1, matrix products, body(): jnp.einsum('swgji,sgip->swjp', intersection, blocks, preferred_element_ty...  47.7 us
    all_to_all x1, blocking collectives, body(): lax.all_to_all(outgoing, WALK, split_axis=0, concat_axis=0, tiled=True)  28.1 us
  transfers between devices with their start and end apart: 3, of which 3 were waited for; matrix products, arithmetic and copies ran while one was open for 1% of the time, Pallas kernels for 0%

profile of v1, /device:TPU:0, one launch (start us, length us, event | category | flops | bytes accessed | tf_op | source)
XLA Modules:
  0.0 539.6 jit_solution(16381691002898503188)
XLA Ops:
  0.6 0.7 and_select_fusion.1
  1.3 0.2 convert_reduce_fusion.1
  1.5 0.1 select_reduce_fusion
  1.6 0.7 sub.11
  2.3 4.6 all-to-all-start
  6.8 1.8 copy.35
  8.6 3.5 all-to-all-done
  12.1 0.1 copy.20
  12.2 10.2 %all_to_all.25 = s32[4,2,1,2]{0,3,2,1:T(2,128)S(1)} all-to-all(s32[4,2,1,2]{0,3,2,1:T(2,128)S(1)} %copy.20), channel_id=1, replica_groups=mesh['walk_0'=4,'walk_1'=2,'chol'=16] {'walk_1'}, dimensions={1} | all-to-all | bytes 128 | tf_op jit(solution)/shard_map/all_to_all | solution.py:27
  22.5 0.1 copy.21
  22.6 0.1 eq.84
  22.6 0.8 convolution_convert_fusion
  23.4 1.2 copy.36
  24.6 28.1 %all_to_all.26 = bf16[8,2,64,1024]{3,2,1,0:T(8,128)(2,1)S(1)} all-to-all(bf16[8,2,64,1024]{3,2,1,0:T(8,128)(2,1)S(1)} %bitcast.85), channel_id=1, replica_groups=mesh['walk_0'=4,'walk_1'=2,'chol'=16] {'walk_0','walk_1'}, dimensions={0} | all-to-all | bytes 4194304 | tf_op jit(solution)/shard_map/all_to_all | solution.py:58
  52.7 8.5 %stack.2 = bf16[16,12,64,1024]{3,2,1,0:T(8,128)(2,1)} broadcast(bf16[12,64,1024]{2,1,0:T(8,128)(2,1)S(1)} %copy-done), dimensions={1,2,3} | broadcast | bytes 26738688 | tf_op jit(solution)/shard_map/stack | solution.py:67
  61.2 5.7 %all-to-all-start.3 = ((bf16[16,12,64,1024]{3,2,1,0:T(8,128)(2,1)}), bf16[16,12,64,1024]{3,2,1,0:T(8,128)(2,1)}, u32[]{:S(2)}, u32[]{:S(2)}) async-start(bf16[16,12,64,1024]{3,2,1,0:T(8,128)(2,1)} %stack.2), calls=%async_computation.3 | async-start | bytes 50331648 | tf_op jit(solution)/shard_map/all_to_all | solution.py:67
  66.9 0.2 convert_bitcast_fusion
  67.1 1.2 copy.38
  69.0 1.2 copy.37
  70.2 0.5 fusion
  70.7 332.6 %all-to-all-done.3 = bf16[16,12,64,1024]{3,2,1,0:T(8,128)(2,1)} async-done(((bf16[16,12,64,1024]{3,2,1,0:T(8,128)(2,1)}), bf16[16,12,64,1024]{3,2,1,0:T(8,128)(2,1)}, u32[]{:S(2)}, u32[]{:S(2)}) %all-to-all-start.3) | async-done | bytes 25165856 | tf_op jit(solution)/shard_map/all_to_all | solution.py:67
  403.3 47.7 %fusion.1 = bf16[16,8,64,1024]{3,2,1,0:T(8,128)(2,1)} fusion(bf16[16,12,64,1024]{3,2,1,0:T(8,128)(2,1)} %all-to-all-done.3, bf16[8,64,1024,1,1]{2,0,1,4,3:T(8,128)(2,1)S(1)} %bitcast.87), kind=kOutput, calls=%fused_computation.4 | convolution fusion | flops 25792872448 | bytes 42991616 | tf_op jit(solution)/shard_map/swgji,sgip->swjp/dot_general | solution.py:74
  451.0 7.3 %convert_reduce_fusion = f32[8,64,1024]{2,1,0:T(8,128)S(1)} fusion(bf16[16,8,64,1024]{3,2,1,0:T(8,128)(2,1)} %fusion.1), kind=kLoop, calls=%fused_computation.5 | loop fusion | flops 16252928 | bytes 18874368 | tf_op jit(solution)/shard_map/reduce_sum | solution.py:76
  458.4 1.2 copy.39
  459.6 0.9 multiply_reduce_fusion
  460.5 1.8 fusion.21
  462.4 4.4 copy.24
  466.8 4.5 all-to-all-start.4
  471.3 0.5 broadcast_multiply_fusion.1
  471.9 59.3 %all-to-all-done.4 = f32[8,2,64,1024]{3,2,1,0:T(8,128)} async-done(((f32[8,2,64,1024]{3,2,1,0:T(8,128)}), f32[8,2,64,1024]{3,2,1,0:T(8,128)}, u32[]{:S(2)}, u32[]{:S(2)}) %all-to-all-start.4) | async-done | bytes 4194336 | tf_op jit(solution)/shard_map/all_to_all | solution.py:86
  531.2 5.9 %fusion.16 = f32[8,64,1024]{2,0,1:T(8,128)S(1)} fusion(s32[16]{0:T(128)S(1)} %eq.84, f32[2,8,64,1024]{3,2,1,0:T(8,128)} %bitcast.37), kind=kOutput, calls=%fused_computation.12 | convolution fusion | flops 100663424 | bytes 6291520 | tf_op jit(solution)/shard_map/dot_general | solution.py:88
  537.0 2.5 copy.26
  (8 shorter events, 0.0 us)
Async XLA Ops:
  2.3 9.9 %all-to-all-start = ((s32[4,2,1,2]{3,1,2,0:T(2,128)}), s32[4,2,1,2]{3,1,2,0:T(2,128)S(1)}, u32[]{:S(2)}, u32[]{:S(2)}) async-start(s32[4,2,1,2]{3,1,2,0:T(2,128)} %bitcast), calls=%async_computation | async-start | bytes 8192 | tf_op jit(solution)/shard_map/all_to_all | solution.py:27
  24.6 28.1 %copy-start = (bf16[12,64,1024]{2,1,0:T(8,128)(2,1)S(1)}, bf16[12,64,1024]{2,1,0:T(8,128)(2,1)}, u32[]{:S(2)}) copy-start(bf16[12,64,1024]{2,1,0:T(8,128)(2,1)} %param.6) | copy-start | bytes 4718596
  61.2 5.7 %copy-start.1 = (bf16[8,64,1024]{2,1,0:T(8,128)(2,1)S(1)}, bf16[8,64,1024]{2,1,0:T(8,128)(2,1)}, u32[]{:S(2)}) copy-start(bf16[8,64,1024]{2,1,0:T(8,128)(2,1)} %param.9) | copy-start | bytes 3145732
  61.2 342.1 %all-to-all-start.3 = ((bf16[16,12,64,1024]{3,2,1,0:T(8,128)(2,1)}), bf16[16,12,64,1024]{3,2,1,0:T(8,128)(2,1)}, u32[]{:S(2)}, u32[]{:S(2)}) async-start(bf16[16,12,64,1024]{3,2,1,0:T(8,128)(2,1)} %stack.2), calls=%async_computation.3 | async-start | bytes 50331648 | tf_op jit(solution)/shard_map/all_to_all | solution.py:67
  466.8 64.4 %all-to-all-start.4 = ((f32[8,2,64,1024]{3,2,1,0:T(8,128)}), f32[8,2,64,1024]{3,2,1,0:T(8,128)}, u32[]{:S(2)}, u32[]{:S(2)}) async-start(f32[8,2,64,1024]{3,2,1,0:T(8,128)} %copy.24), calls=%async_computation.4 | async-start | bytes 8388608 | tf_op jit(solution)/shard_map/all_to_all | solution.py:86
